TPU v7x, 32 devices: a whole 2x2x4 slice. The times are simulated.
32 devices in a mesh: blk: 16 (over z, y, core), grp: 2 (over x).
Axes of the slice: x: 2, y: 2, z: 4, core: 2. Of those that a mesh axis runs over, the one named last changes fastest.
Arguments:
- matrix_sat: float32 [512, 65536], P('grp', 'blk'), may hold values from -0.07883404 to 0.07883404
- matrix_ter: float32 [512, 65536], P('grp', 'blk'), may hold values from -0.07883404 to 0.07883404
- probes: float32 [16, 65536], P(None, 'blk'), may hold values from -6 to 6
Outputs:
- row_part: float32 [2, 16, 512], P(None, None, 'grp')
- column_part: float32 [2, 16, 65536], P(None, None, ('blk', 'grp'))
- trace_terms: float32 [2, 16], replicated
All inputs are finite; a program needn't handle non-finite values.
Results may differ from a plain program's by a relative error of at most 0.000096.
Values sent between devices are 32-bit elements; how exact they have to be, the bound alone decides.
A program may use at most 64 MiB of HBM per device.

v0:
```python
import jax
import jax.numpy as jnp
from jax import lax
from jax.sharding import PartitionSpec as P


def broadcast(block, axis, source):
    block = jnp.where(lax.axis_index(axis) == source, block, jnp.zeros_like(block))
    return lax.psum(block, axis)


def shards(matrix_sat, matrix_ter, probes):
    rows_dev, cols_dev = matrix_sat.shape
    column_index = lax.axis_index("blk")
    row_index = lax.axis_index("grp")
    row_ids = row_index * rows_dev + lax.broadcasted_iota(jnp.int32, (rows_dev, cols_dev), 0)
    col_ids = column_index * cols_dev + lax.broadcasted_iota(jnp.int32, (rows_dev, cols_dev), 1)
    upper_mask = col_ids >= row_ids
    strict_mask = col_ids > row_ids
    mine = lax.dynamic_slice_in_dim(probes, row_index * rows_dev, rows_dev, 1)
    slab_probes = broadcast(mine, "blk", 0)
    hp = lax.Precision.HIGHEST
    direct_list = []
    mirror_list = []
    for matrix in (matrix_sat, matrix_ter):
        masked_upper = jnp.where(upper_mask, matrix, 0.0)
        masked_strict = jnp.where(strict_mask, matrix, 0.0)
        direct_list.append(
            lax.dot_general(probes, masked_upper, (((1,), (1,)), ((), ())), precision=hp)
        )
        mirror_list.append(jnp.dot(slab_probes, masked_strict, precision=hp))
    direct_terms = jnp.stack(direct_list)
    mirror_terms = jnp.stack(mirror_list)
    early_local = jnp.sum(slab_probes[None] * direct_terms, axis=2) + jnp.sum(
        probes[None] * mirror_terms, axis=2
    )
    early_trace = lax.psum(early_local, ("blk", "grp"))
    row_part = lax.psum(direct_terms, "blk")
    column_part = lax.psum_scatter(mirror_terms, "grp", scatter_dimension=2, tiled=True)
    return (row_part, column_part, early_trace)


def solution(mesh):
    in_specs = (P("grp", "blk"), P("grp", "blk"), P(None, "blk"))
    out_specs = (P(None, None, "grp"), P(None, None, ("blk", "grp")), P())
    return jax.shard_map(shards, mesh=mesh, in_specs=in_specs, out_specs=out_specs, check_vma=False)
```

profile of v0, /device:TPU:14, one launch (start us, length us, event | category | flops | bytes accessed | tf_op | source)
XLA Modules:
  0.0 133.0 jit_solution(6201908092485074033)
XLA Ops:
  7.2 0.0 copy-start.2
  7.2 0.0 reduce-scatter.2.cloned.1.call-start
  7.2 0.0 copy-start
  7.3 5.8 %fusion.14 = f32[1,16,256]{2,1,0:T(8,128)S(1)} fusion(f32[16,4096]{1,0:T(8,128)} %param.5, f32[256,4096]{1,0:T(8,128)} %param.4, s32[4096]{0:T(1024)S(1)} %iota_add_fusion, s32[256]{0:T(256)S(1)} %iota_add_fusion.1), kind=kOutput, calls=%fused_computation.20 | convolution fusion | flops 203423744 | bytes 4490240 | tf_op jit(solution)/shard_map/dot_general | solution.py:29
  13.1 0.0 copy-done.2
  13.1 0.0 copy-done
  13.1 3.5 %fusion.15 = f32[1,16,256]{2,1,0:T(8,128)S(1)} fusion(f32[16,4096]{1,0:T(8,128)S(1)} %copy-done.2, f32[256,4096]{1,0:T(8,128)S(1)} %copy-done, s32[4096]{0:T(1024)S(1)} %iota_add_fusion, s32[256]{0:T(256)S(1)} %iota_add_fusion.1), kind=kOutput, calls=%fused_computation.21 | convolution fusion | flops 203423744 | bytes 4490240 | tf_op jit(solution)/shard_map/dot_general | solution.py:29
  16.6 49.1 %all-reduce = (f32[2,16,256]{2,1,0:T(8,128)}, f32[16,256]{1,0:T(8,128)S(1)}) all-reduce(f32[2,16,256]{2,1,0:T(8,128)S(1)} %pad_maximum_fusion.1, f32[16,256]{1,0:T(8,128)S(1)} %dynamic-slice_select_fusion), channel_id=1, replica_groups=mesh['blk'=16,'grp'=2] {'blk'}, use_global_device_ids=true, to_apply=%region_0.1 | all-reduce | flops 12288 | bytes 98304 | tf_op jit(solution)/shard_map/psum | solution.py:38
  65.7 0.0 copy-start.1
  65.7 4.7 %convolution_bitcast_fusion = f32[1,16,4096]{2,1,0:T(8,128)S(1)} fusion(f32[16,256]{1,0:T(8,128)S(1)} %get-tuple-element.4, f32[256,4096]{1,0:T(8,128)} %param.4, s32[4096]{0:T(1024)S(1)} %iota_add_fusion, s32[256]{0:T(256)S(1)} %iota_add_fusion.1), kind=kOutput, calls=%fused_computation.4 | convolution fusion | flops 203423744 | bytes 4490240 | tf_op jit(solution)/shard_map/dot_general | solution.py:31
  70.4 0.0 copy-done.1
  70.4 2.4 %convolution_bitcast_fusion.1 = f32[1,16,4096]{2,1,0:T(8,128)S(1)} fusion(f32[16,256]{1,0:T(8,128)S(1)} %get-tuple-element.4, f32[256,4096]{1,0:T(8,128)S(1)} %copy-done.1, s32[4096]{0:T(1024)S(1)} %iota_add_fusion, s32[256]{0:T(256)S(1)} %iota_add_fusion.1), kind=kOutput, calls=%fused_computation.5 | convolution fusion | flops 203423744 | bytes 4490240 | tf_op jit(solution)/shard_map/dot_general | solution.py:31
  72.8 0.9 multiply_reduce_fusion
  73.7 0.0 reduce-scatter.2.cloned.1.call-update
  73.7 0.1 multiply_reduce_fusion.1
  73.8 52.4 %psum.23 = f32[2,16]{1,0:T(2,128)} all-reduce(f32[2,16]{1,0:T(2,128)S(1)} %add.33), channel_id=1, replica_groups=mesh['blk'=16,'grp'=2] {'blk','grp'}, use_global_device_ids=true, to_apply=%region_5.6 | all-reduce | flops 32 | bytes 256 | tf_op jit(solution)/shard_map/psum | solution.py:37
  126.2 0.0 reduce-scatter.2.cloned.1.call-done
  (5 shorter events, 0.0 us)
Async XLA Ops:
  7.2 5.9 %copy-start.2 = (f32[16,4096]{1,0:T(8,128)S(1)}, f32[16,4096]{1,0:T(8,128)}, u32[]{:S(2)}) copy-start(f32[16,4096]{1,0:T(8,128)} %param.5) | copy-start | bytes 786436
  7.2 119.0 %reduce-scatter.2.cloned.1.call-start = ((), (), s32[]{:S(2)}) async-start(), calls=%async_computation.1 | async-start | bytes 786432 | tf_op jit(solution)/shard_map/reduce_scatter | solution.py:39
  7.2 5.9 %copy-start = (f32[256,4096]{1,0:T(8,128)S(1)}, f32[256,4096]{1,0:T(8,128)}, u32[]{:S(2)}) copy-start(f32[256,4096]{1,0:T(8,128)} %param.3) | copy-start | bytes 12582916
  65.7 4.7 %copy-start.1 = (f32[256,4096]{1,0:T(8,128)S(1)}, f32[256,4096]{1,0:T(8,128)}, u32[]{:S(2)}) copy-start(f32[256,4096]{1,0:T(8,128)} %param.3) | copy-start | bytes 12582916
Sparse Core Ops, SparseCore 0:
  73.8 24.2 reduce-scatter.1
where the time goes:
time: 133 us
  blocking collectives  101 us (76%)
  matrix products  16.3 us (12%)
  between operations  14.1 us (11%)
    psum x1, blocking collectives, shards(): early_trace = lax.psum(early_local, ('blk', 'grp'))  52.4 us
    psum x1, blocking collectives, shards(): row_part = lax.psum(direct_terms, 'blk')  49.1 us
    dot_general x2, matrix products, shards(): lax.dot_general(probes, masked_upper, (((1,), (1,)), ((), ())), precision...  9.25 us
    dot_general x2, matrix products, shards(): mirror_list.append(jnp.dot(slab_probes, masked_strict, precision=hp))  7.08 us
  transfers between devices with their start and end apart: 1, of which 0 were waited for; matrix products, arithmetic and copies ran while one was open for 0% of the time, Pallas kernels for 0%

commit v1 on v0

--- a/solution.py
+++ b/solution.py
@@ -34,7 +34,7 @@
     early_local = jnp.sum(slab_probes[None] * direct_terms, axis=2) + jnp.sum(
         probes[None] * mirror_terms, axis=2
     )
-    early_trace = lax.psum(early_local, ("blk", "grp"))
+    early_trace = jnp.sum(lax.all_gather(early_local, ("blk", "grp")), axis=0)
     row_part = lax.psum(direct_terms, "blk")
     column_part = lax.psum_scatter(mirror_terms, "grp", scatter_dimension=2, tiled=True)
     return (row_part, column_part, early_trace)

time: 133 us -> 161 us (1.21)
  the two profiles are of different devices: /device:TPU:14 before, /device:TPU:0 now
where the time goes in v1:
time: 161 us
  blocking collectives  129 us (80%)
  matrix products  16.3 us (10%)
  between operations  14.1 us (9%)
    all_gather x1, blocking collectives, shards(): early_trace = jnp.sum(lax.all_gather(early_local, ('blk', 'grp')), axis=0)  64.9 us
    psum x1, blocking collectives, shards(): row_part = lax.psum(direct_terms, 'blk')  63.7 us
    dot_general x2, matrix products, shards(): lax.dot_general(probes, masked_upper, (((1,), (1,)), ((), ())), precision...  9.25 us
    dot_general x2, matrix products, shards(): mirror_list.append(jnp.dot(slab_probes, masked_strict, precision=hp))  7.08 us
  transfers between devices with their start and end apart: 1, of which 0 were waited for; matrix products, arithmetic and copies ran while one was open for 0% of the time, Pallas kernels for 0%

profile of v1, /device:TPU:0, one launch (start us, length us, event | category | flops | bytes accessed | tf_op | source)
XLA Modules:
  0.0 160.7 jit_solution(2774519723042225702)
XLA Ops:
  7.2 0.0 copy-start.2
  7.2 0.0 reduce-scatter.2.cloned.1.call-start
  7.2 0.0 copy-start
  7.3 5.8 %fusion.14 = f32[1,16,256]{2,1,0:T(8,128)S(1)} fusion(f32[16,4096]{1,0:T(8,128)} %param.5, f32[256,4096]{1,0:T(8,128)} %param.4, s32[4096]{0:T(1024)S(1)} %iota_add_fusion, s32[256]{0:T(256)S(1)} %iota_add_fusion.1), kind=kOutput, calls=%fused_computation.20 | convolution fusion | flops 203423744 | bytes 4490240 | tf_op jit(solution)/shard_map/dot_general | solution.py:29
  13.1 0.0 copy-done.2
  13.1 0.0 copy-done
  13.1 3.5 %fusion.15 = f32[1,16,256]{2,1,0:T(8,128)S(1)} fusion(f32[16,4096]{1,0:T(8,128)S(1)} %copy-done.2, f32[256,4096]{1,0:T(8,128)S(1)} %copy-done, s32[4096]{0:T(1024)S(1)} %iota_add_fusion, s32[256]{0:T(256)S(1)} %iota_add_fusion.1), kind=kOutput, calls=%fused_computation.21 | convolution fusion | flops 203423744 | bytes 4490240 | tf_op jit(solution)/shard_map/dot_general | solution.py:29
  16.6 63.7 %all-reduce = (f32[2,16,256]{2,1,0:T(8,128)}, f32[16,256]{1,0:T(8,128)S(1)}) all-reduce(f32[2,16,256]{2,1,0:T(8,128)S(1)} %pad_maximum_fusion.1, f32[16,256]{1,0:T(8,128)S(1)} %dynamic-slice_select_fusion), channel_id=1, replica_groups=mesh['blk'=16,'grp'=2] {'blk'}, use_global_device_ids=true, to_apply=%region_0.1 | all-reduce | flops 12288 | bytes 98304 | tf_op jit(solution)/shard_map/psum | solution.py:38
  80.3 0.0 copy-start.1
  80.3 4.7 %convolution_bitcast_fusion = f32[1,16,4096]{2,1,0:T(8,128)S(1)} fusion(f32[16,256]{1,0:T(8,128)S(1)} %get-tuple-element.4, f32[256,4096]{1,0:T(8,128)} %param.4, s32[4096]{0:T(1024)S(1)} %iota_add_fusion, s32[256]{0:T(256)S(1)} %iota_add_fusion.1), kind=kOutput, calls=%fused_computation.4 | convolution fusion | flops 203423744 | bytes 4490240 | tf_op jit(solution)/shard_map/dot_general | solution.py:31
  85.0 0.0 copy-done.1
  85.0 2.4 %convolution_bitcast_fusion.1 = f32[1,16,4096]{2,1,0:T(8,128)S(1)} fusion(f32[16,256]{1,0:T(8,128)S(1)} %get-tuple-element.4, f32[256,4096]{1,0:T(8,128)S(1)} %copy-done.1, s32[4096]{0:T(1024)S(1)} %iota_add_fusion, s32[256]{0:T(256)S(1)} %iota_add_fusion.1), kind=kOutput, calls=%fused_computation.5 | convolution fusion | flops 203423744 | bytes 4490240 | tf_op jit(solution)/shard_map/dot_general | solution.py:31
  87.4 0.9 multiply_reduce_fusion
  88.2 0.0 reduce-scatter.2.cloned.1.call-update
  88.2 0.1 multiply_reduce_fusion.1
  88.3 64.9 %all-gather.1 = f32[32,2,16]{2,1,0:T(2,128)S(1)} all-gather(f32[1,2,16]{2,1,0:T(2,128)S(1)} %add_bitcast_fusion), channel_id=2, replica_groups=mesh['blk'=16,'grp'=2] {'blk','grp'}, dimensions={0}, use_global_device_ids=true | all-gather | bytes 4224 | tf_op jit(solution)/shard_map/all_gather | solution.py:37
  153.3 0.6 reduce_sum.29
  153.9 0.0 reduce-scatter.2.cloned.1.call-done
  (5 shorter events, 0.0 us)
Async XLA Ops:
  7.2 5.9 %copy-start.2 = (f32[16,4096]{1,0:T(8,128)S(1)}, f32[16,4096]{1,0:T(8,128)}, u32[]{:S(2)}) copy-start(f32[16,4096]{1,0:T(8,128)} %param.5) | copy-start | bytes 786436
  7.2 146.7 %reduce-scatter.2.cloned.1.call-start = ((), (), s32[]{:S(2)}) async-start(), calls=%async_computation.1 | async-start | bytes 786432 | tf_op jit(solution)/shard_map/reduce_scatter | solution.py:39
  7.2 5.9 %copy-start = (f32[256,4096]{1,0:T(8,128)S(1)}, f32[256,4096]{1,0:T(8,128)}, u32[]{:S(2)}) copy-start(f32[256,4096]{1,0:T(8,128)} %param.3) | copy-start | bytes 12582916
  80.3 4.7 %copy-start.1 = (f32[256,4096]{1,0:T(8,128)S(1)}, f32[256,4096]{1,0:T(8,128)}, u32[]{:S(2)}) copy-start(f32[256,4096]{1,0:T(8,128)} %param.3) | copy-start | bytes 12582916
Sparse Core Ops, SparseCore 0:
  88.4 11.9 reduce-scatter.1
